TPU v7x, 256 devices: a whole 4x4x8 slice. The times are simulated.
256 devices in a mesh: dp: 8 (over z), feat: 32 (over x, y, core).
Axes of the slice: x: 4, y: 4, z: 8, core: 2. Of those that a mesh axis runs over, the one named last changes fastest.
Arguments:
- features: float32 [8192, 32768], P('dp', 'feat'), may hold values from -0.03125 to 0.03125
- labels: int32 [8192], P('dp'), may hold values from -1 to 1, as said below
- weights: float32 [32768], P('feat'), may hold values from -6 to 6
Outputs:
- gradient: float32 [32768], P('feat')
- newton_step: float32 [32768], P('feat')
- residual: float32 [32768], P('feat')
Inputs may be any that keep to these rules, and one draw needn't show every extreme that they name: `labels`: every label is -1 or +1.
All inputs are finite; a program needn't handle non-finite values.
Results may differ from a plain program's by a relative error of at most 0.0003.
Values sent between devices are 32-bit elements; how exact they have to be, the bound alone decides.
A program may use at most 64 MiB of HBM per device.

v0:
```python
import jax
import jax.numpy as jnp
from jax import lax
from jax.sharding import PartitionSpec as P

CG_STEPS = 3


PENALTY = 4.0
HIGH = lax.Precision.HIGHEST


def sent_to_all(value, axis):
    count = lax.axis_size(axis)
    return lax.all_to_all(
        jnp.broadcast_to(value[None], (count, *value.shape)), axis, 0, 0, tiled=True
    )


def over_copies(value, axis):
    return sent_to_all(value, axis).sum(axis=0)


def together(arrays, axis):
    flat, at, finished = (jnp.concatenate([a.reshape(-1) for a in arrays]), 0, [])
    subtotal = over_copies(flat, axis)
    for a in arrays:
        finished.append(subtotal[at : at + a.size].reshape(a.shape))
        at += a.size
    return tuple(finished)


def squares(residual):
    return over_copies(jnp.sum(residual * residual), "feat")


def local(features, labels, weights):
    y = labels.astype(jnp.float32)
    margin = y * over_copies(jnp.dot(features, weights, precision=HIGH), "feat")
    sig = 1.0 / (1.0 + jnp.exp(-margin))
    local_grad = jnp.dot((sig - 1.0) * y, features, precision=HIGH)
    gradient = weights + PENALTY * over_copies(local_grad, "dp")
    curv = PENALTY * sig * (1.0 - sig)
    newton_step = jnp.zeros_like(weights)
    residual = -gradient
    direction = residual
    rr = squares(residual)
    for step in range(CG_STEPS):
        image_rows, dir_sq = together(
            (jnp.dot(features, direction, precision=HIGH), jnp.sum(direction * direction)), "feat"
        )
        weighted = curv * image_rows
        back, quad = together(
            (jnp.dot(weighted, features, precision=HIGH), jnp.sum(weighted * image_rows)), "dp"
        )
        curvature = dir_sq + quad
        image = direction + back
        alpha = rr / curvature
        newton_step = newton_step + alpha * direction
        residual = residual - alpha * image
        fresh = squares(residual)
        direction = residual + fresh / rr * direction
        rr = fresh
    return (gradient, newton_step, residual)


def solution(mesh):
    placed = (P("dp", "feat"), P("dp"), P("feat"))
    return jax.shard_map(
        local,
        mesh=mesh,
        in_specs=placed,
        out_specs=(P("feat"), P("feat"), P("feat")),
        check_vma=False,
    )
```

profile of v0, /device:TPU:1, one launch (start us, length us, event | category | flops | bytes accessed | tf_op | source)
XLA Modules:
  0.0 195.6 jit_solution(6194294434217252378)
XLA Ops:
  0.7 5.8 %fusion.8 = f32[1,1024]{1,0:T(1,128)S(1)} fusion(f32[1024,1024]{1,0:T(8,128)} %param.3, f32[1024,1]{0,1:T(1,128)} %bitcast.52), kind=kOutput, calls=%fused_computation.34 | convolution fusion | flops 12582912 | bytes 4202496 | tf_op jit(solution)/shard_map/dot_general | solution.py:39
  6.5 16.1 %all_to_all.66 = f32[32,1,1024]{2,1,0:T(1,128)S(1)} all-to-all(f32[32,1,1024]{2,1,0:T(1,128)S(1)} %broadcast_in_dim.24), channel_id=1, replica_groups=mesh['dp'=8,'feat'=32] {'feat'}, dimensions={0} | all-to-all | bytes 262144 | tf_op jit(solution)/shard_map/all_to_all | solution.py:15
  22.7 4.3 %fusion.9 = f32[1,1024]{1,0:T(1,128)S(1)} fusion(f32[1024,1]{0,1:T(1,128)S(1)} %bitcast.51, f32[1024,1024]{1,0:T(8,128)} %param.3), kind=kOutput, calls=%fused_computation.35 | convolution fusion | flops 12582912 | bytes 4202496 | tf_op jit(solution)/shard_map/dot_general | solution.py:41
  27.0 15.0 %all_to_all.67 = f32[8,1,1024]{2,1,0:T(1,128)S(1)} all-to-all(f32[8,1,1024]{2,1,0:T(1,128)S(1)} %broadcast_in_dim.25), channel_id=1, replica_groups=mesh['dp'=8,'feat'=32] {'dp'}, dimensions={0} | all-to-all | bytes 65536 | tf_op jit(solution)/shard_map/all_to_all | solution.py:15
  42.6 5.6 %fusion.10 = f32[1,1024]{1,0:T(1,128)S(1)} fusion(f32[1024,1]{0,1:T(1,128)S(1)} %bitcast.53, f32[1024,1024]{1,0:T(8,128)} %param.3), kind=kOutput, calls=%fused_computation.36 | convolution fusion | flops 12582912 | bytes 4202496 | tf_op jit(solution)/shard_map/dot_general | solution.py:50
  48.2 0.7 pad_maximum_fusion
  49.0 12.7 %all_to_all.68 = f32[32,1,1025]{2,1,0:T(1,128)S(1)} all-to-all(f32[32,1,1025]{2,1,0:T(1,128)S(1)} %broadcast_in_dim.28), channel_id=1, replica_groups=mesh['dp'=8,'feat'=32] {'feat'}, dimensions={0} | all-to-all | bytes 262400 | tf_op jit(solution)/shard_map/all_to_all | solution.py:15
  61.7 1.2 broadcast_in_dim.26
  63.0 3.9 %all-to-all-start.2 = ((f32[32,1,1]{2,1,0:T(1,128)}), f32[32,1,1]{2,1,0:T(1,128)S(1)}, u32[]{:S(2)}, u32[]{:S(2)}) async-start(f32[32,1,1]{2,1,0:T(1,128)} %broadcast_in_dim.26), calls=%async_computation.2 | async-start | bytes 32768 | tf_op jit(solution)/shard_map/all_to_all | solution.py:15
  67.6 4.3 %fusion.11 = f32[1,1024]{1,0:T(1,128)S(1)} fusion(f32[1024,1]{0,1:T(1,128)S(1)} %bitcast.55, f32[1024,1024]{1,0:T(8,128)} %param.3), kind=kOutput, calls=%fused_computation.37 | convolution fusion | flops 12582912 | bytes 4202496 | tf_op jit(solution)/shard_map/dot_general | solution.py:54
  71.9 0.6 pad_maximum_fusion.1
  72.5 1.4 all-to-all-done.2
  74.6 3.5 %all-to-all-start.4 = ((f32[8,1,1025]{2,1,0:T(1,128)}), f32[8,1,1025]{2,1,0:T(1,128)S(1)}, u32[]{:S(2)}, u32[]{:S(2)}) async-start(f32[8,1,1025]{2,1,0:T(1,128)} %broadcast_in_dim.29), calls=%async_computation.4 | async-start | bytes 73728 | tf_op jit(solution)/shard_map/all_to_all | solution.py:15
  79.3 5.8 %all-to-all-done.4 = f32[8,1,1025]{2,1,0:T(1,128)S(1)} async-done(((f32[8,1,1025]{2,1,0:T(1,128)}), f32[8,1,1025]{2,1,0:T(1,128)S(1)}, u32[]{:S(2)}, u32[]{:S(2)}) %all-to-all-start.4) | async-done | bytes 32832 | tf_op jit(solution)/shard_map/all_to_all | solution.py:15
  88.3 0.7 broadcast_in_dim.30
  88.9 13.9 %all_to_all.69 = f32[32,1,1]{2,1,0:T(1,128)S(1)} all-to-all(f32[32,1,1]{2,1,0:T(1,128)S(1)} %broadcast_in_dim.30), channel_id=1, replica_groups=mesh['dp'=8,'feat'=32] {'feat'}, dimensions={0} | all-to-all | bytes 256 | tf_op jit(solution)/shard_map/all_to_all | solution.py:15
  105.4 5.6 %fusion.12 = f32[1,1024]{1,0:T(1,128)S(1)} fusion(f32[1024,1]{0,1:T(1,128)S(1)} %bitcast.41, f32[1024,1024]{1,0:T(8,128)} %param.3), kind=kOutput, calls=%fused_computation.38 | convolution fusion | flops 12582912 | bytes 4202496 | tf_op jit(solution)/shard_map/dot_general | solution.py:50
  111.1 0.7 pad_maximum_fusion.2
  111.8 11.5 %all_to_all.70 = f32[32,1,1025]{2,1,0:T(1,128)S(1)} all-to-all(f32[32,1,1025]{2,1,0:T(1,128)S(1)} %broadcast_in_dim.31), channel_id=1, replica_groups=mesh['dp'=8,'feat'=32] {'feat'}, dimensions={0} | all-to-all | bytes 262400 | tf_op jit(solution)/shard_map/all_to_all | solution.py:15
  124.1 4.3 %fusion.13 = f32[1,1024]{1,0:T(1,128)S(1)} fusion(f32[1024,1]{0,1:T(1,128)S(1)} %bitcast.56, f32[1024,1024]{1,0:T(8,128)} %param.3), kind=kOutput, calls=%fused_computation.39 | convolution fusion | flops 12582912 | bytes 4202496 | tf_op jit(solution)/shard_map/dot_general | solution.py:54
  128.3 0.6 pad_maximum_fusion.3
  129.6 3.3 %all-to-all-start.7 = ((f32[8,1,1025]{2,1,0:T(1,128)}), f32[8,1,1025]{2,1,0:T(1,128)S(1)}, u32[]{:S(2)}, u32[]{:S(2)}) async-start(f32[8,1,1025]{2,1,0:T(1,128)} %broadcast_in_dim.32), calls=%async_computation.7 | async-start | bytes 73728 | tf_op jit(solution)/shard_map/all_to_all | solution.py:15
  133.5 6.3 %all-to-all-done.7 = f32[8,1,1025]{2,1,0:T(1,128)S(1)} async-done(((f32[8,1,1025]{2,1,0:T(1,128)}), f32[8,1,1025]{2,1,0:T(1,128)S(1)}, u32[]{:S(2)}, u32[]{:S(2)}) %all-to-all-start.7) | async-done | bytes 32832 | tf_op jit(solution)/shard_map/all_to_all | solution.py:15
  143.0 0.7 broadcast_in_dim.33
  143.7 11.7 %all_to_all.71 = f32[32,1,1]{2,1,0:T(1,128)S(1)} all-to-all(f32[32,1,1]{2,1,0:T(1,128)S(1)} %broadcast_in_dim.33), channel_id=1, replica_groups=mesh['dp'=8,'feat'=32] {'feat'}, dimensions={0} | all-to-all | bytes 256 | tf_op jit(solution)/shard_map/all_to_all | solution.py:15
  158.0 5.6 %fusion.14 = f32[1,1024]{1,0:T(1,128)S(1)} fusion(f32[1024,1]{0,1:T(1,128)S(1)} %bitcast.42, f32[1024,1024]{1,0:T(8,128)} %param.3), kind=kOutput, calls=%fused_computation.40 | convolution fusion | flops 12582912 | bytes 4202496 | tf_op jit(solution)/shard_map/dot_general | solution.py:50
  163.6 0.7 pad_maximum_fusion.4
  164.4 11.5 %all_to_all.72 = f32[32,1,1025]{2,1,0:T(1,128)S(1)} all-to-all(f32[32,1,1025]{2,1,0:T(1,128)S(1)} %broadcast_in_dim.34), channel_id=1, replica_groups=mesh['dp'=8,'feat'=32] {'feat'}, dimensions={0} | all-to-all | bytes 262400 | tf_op jit(solution)/shard_map/all_to_all | solution.py:15
  176.6 4.3 %fusion.15 = f32[1,1024]{1,0:T(1,128)S(1)} fusion(f32[1024,1]{0,1:T(1,128)S(1)} %bitcast.54, f32[1024,1024]{1,0:T(8,128)} %param.3), kind=kOutput, calls=%fused_computation.41 | convolution fusion | flops 12582912 | bytes 4202496 | tf_op jit(solution)/shard_map/dot_general | solution.py:54
  180.9 0.6 pad_maximum_fusion.5
  182.2 3.3 %all-to-all-start.10 = ((f32[8,1,1025]{2,1,0:T(1,128)}), f32[8,1,1025]{2,1,0:T(1,128)S(1)}, u32[]{:S(2)}, u32[]{:S(2)}) async-start(f32[8,1,1025]{2,1,0:T(1,128)} %broadcast_in_dim.35), calls=%async_computation.10 | async-start | bytes 73728 | tf_op jit(solution)/shard_map/all_to_all | solution.py:15
  186.0 6.3 %all-to-all-done.10 = f32[8,1,1025]{2,1,0:T(1,128)S(1)} async-done(((f32[8,1,1025]{2,1,0:T(1,128)}), f32[8,1,1025]{2,1,0:T(1,128)S(1)}, u32[]{:S(2)}, u32[]{:S(2)}) %all-to-all-start.10) | async-done | bytes 32832 | tf_op jit(solution)/shard_map/all_to_all | solution.py:15
  (42 shorter events, 13.5 us)
Async XLA Ops:
  0.6 22.0 %copy-start.1 = (s32[1024]{0:T(1024)S(1)}, s32[1024]{0:T(1024)}, u32[]{:S(2)}) copy-start(s32[1024]{0:T(1024)} %param.4) | copy-start | bytes 12292
  0.6 41.3 %copy-start.2 = (f32[1024]{0:T(1024)S(1)}, f32[1024]{0:T(1024)}, u32[]{:S(2)}) copy-start(f32[1024]{0:T(1024)} %param.5) | copy-start | bytes 12292
  42.0 153.0 %copy-start = (f32[1024]{0:T(1024)}, f32[1024]{0:T(1024)S(1)}, u32[]{:S(2)}) copy-start(f32[1024]{0:T(1024)S(1)} %get-tuple-element.16) | copy-start | bytes 12292
  63.0 11.0 %all-to-all-start.2 = ((f32[32,1,1]{2,1,0:T(1,128)}), f32[32,1,1]{2,1,0:T(1,128)S(1)}, u32[]{:S(2)}, u32[]{:S(2)}) async-start(f32[32,1,1]{2,1,0:T(1,128)} %broadcast_in_dim.26), calls=%async_computation.2 | async-start | bytes 32768 | tf_op jit(solution)/shard_map/all_to_all | solution.py:15
  74.6 10.4 %all-to-all-start.4 = ((f32[8,1,1025]{2,1,0:T(1,128)}), f32[8,1,1025]{2,1,0:T(1,128)S(1)}, u32[]{:S(2)}, u32[]{:S(2)}) async-start(f32[8,1,1025]{2,1,0:T(1,128)} %broadcast_in_dim.29), calls=%async_computation.4 | async-start | bytes 73728 | tf_op jit(solution)/shard_map/all_to_all | solution.py:15
  129.6 10.2 %all-to-all-start.7 = ((f32[8,1,1025]{2,1,0:T(1,128)}), f32[8,1,1025]{2,1,0:T(1,128)S(1)}, u32[]{:S(2)}, u32[]{:S(2)}) async-start(f32[8,1,1025]{2,1,0:T(1,128)} %broadcast_in_dim.32), calls=%async_computation.7 | async-start | bytes 73728 | tf_op jit(solution)/shard_map/all_to_all | solution.py:15
  182.2 10.2 %all-to-all-start.10 = ((f32[8,1,1025]{2,1,0:T(1,128)}), f32[8,1,1025]{2,1,0:T(1,128)S(1)}, u32[]{:S(2)}, u32[]{:S(2)}) async-start(f32[8,1,1025]{2,1,0:T(1,128)} %broadcast_in_dim.35), calls=%async_computation.10 | async-start | bytes 73728 | tf_op jit(solution)/shard_map/all_to_all | solution.py:15
where the time goes:
time: 197 us; the launch traced here: 196 us
  blocking collectives  92.4 us (47%)
  matrix products  39.8 us (20%)
  waiting for transfers between devices  19.9 us (10%)
  starting transfers between devices  14.1 us (7%)
  other arithmetic  11.9 us (6%)
  between operations  9.5 us (5%)
  local copies, waits for them, and re-layouts  8.1 us (4%)
    all_to_all x7, blocking collectives, sent_to_all(): lax.all_to_all(jnp.broadcast_to(value[None], (count, *value.shape)), axis...  92.4 us
    all_to_all x4, waiting for transfers between devices, sent_to_all(): lax.all_to_all(jnp.broadcast_to(value[None], (count, *value.shape)), axis...  19.9 us
    dot_general x3, matrix products, local(): jnp.dot(features, direction, precision=HIGH)  16.9 us
    all_to_all x4, starting transfers between devices, sent_to_all(): lax.all_to_all(jnp.broadcast_to(value[None], (count, *value.shape)), axis...  14.1 us
    dot_general x3, matrix products, local(): jnp.dot(weighted, features, precision=HIGH)  12.8 us
    dot_general x1, matrix products, local(): margin = y * over_copies(jnp.dot(features, weights, precision=HIGH), 'feat')  5.76 us
    broadcast_in_dim x11, local copies, waits for them, and re-layouts, sent_to_all(): jnp.broadcast_to(value[None], (count, *value.shape))  4.77 us
    dot_general x1, matrix products, local(): local_grad = jnp.dot((sig - 1.0) * y, features, precision=HIGH)  4.27 us
  transfers between devices with their start and end apart: 4, of which 4 were waited for; matrix products, arithmetic and copies ran while one was open for 4% of the time, Pallas kernels for 0%

commit v1 on v0

v1 whole, which is shorter than its diff:
```python
import functools

import jax
import jax.numpy as jnp
from jax import lax
from jax.experimental import pallas as pl
from jax.experimental.pallas import tpu as pltpu
from jax.sharding import PartitionSpec as P

CG_STEPS = 3
PENALTY = 4.0
MESH = pl.DeviceIdType.MESH

N = 1024
LANES = 128
ROWS = N // LANES
CHUNK = 256
NCHUNK = N // CHUNK
NX, NY, NC, NZ = 4, 4, 2, 8
NF = NX * NY * NC
SLOT = 16


def ring(d, n):
    return min(d, n - d)


F_PEERS = sorted(
    ((a, b, c) for a in range(NX) for b in range(NY) for c in range(NC) if (a, b, c) != (0, 0, 0)),
    key=lambda o: (-(ring(o[0], NX) + ring(o[1], NY)), -o[2]),
)
D_PEERS = sorted(range(1, NZ), key=lambda d: -ring(d, NZ))


def kernel(x_hbm, labels_ref, w_ref, grad_ref, step_ref, res_ref,
           xf, xh, xl, fbuf, dbuf, xsem, fs, fr, ds_, dr):
    feat = lax.axis_index("feat")
    z = lax.axis_index("dp")
    px, py, pc = feat // (NY * NC), (feat // NC) % NY, feat % NC

    loads = []
    for c in range(NCHUNK):
        rows = pl.ds(c * CHUNK, CHUNK)
        cp = pltpu.make_async_copy(x_hbm.at[rows], xf.at[rows], xsem.at[c])
        cp.start()
        loads.append(cp)

    def f_id(o):
        return {"feat": (((px + o[0]) % NX) * NY + (py + o[1]) % NY) * NC + (pc + o[2]) % NC}

    def d_id(o):
        return {"dp": (z + o) % NZ}

    barrier = pltpu.get_barrier_semaphore()
    for o in F_PEERS:
        pl.semaphore_signal(barrier, inc=1, device_id=f_id(o), device_id_type=MESH)
    for o in D_PEERS:
        pl.semaphore_signal(barrier, inc=1, device_id=d_id(o), device_id_type=MESH)

    sub = lax.broadcasted_iota(jnp.int32, (ROWS, LANES), 0)

    def lhs_of(v):
        hi = v.astype(jnp.bfloat16).astype(jnp.float32)
        lo = v - hi
        parts = []
        for k in range(ROWS):
            on = sub == k
            parts.append(jnp.concatenate([jnp.where(on, hi, 0.0), jnp.where(on, lo, 0.0)], axis=0).astype(jnp.bfloat16))
        return jnp.concatenate(parts, axis=1)

    def mult(lhs, rhs, dims):
        return lax.dot_general(lhs, rhs, (dims, ((), ())), preferred_element_type=jnp.float32)

    def to_slot(out, ref, base):
        total = jnp.sum(out, axis=0, keepdims=True)
        for k in range(out.shape[1] // LANES):
            ref[pl.ds(base + k, 1), :] = total[:, k * LANES:(k + 1) * LANES]

    def exchange(buf, n, me, count, rows, peers, ident, ssem, rsem, first=False):
        mine = buf.at[n, me, pl.ds(0, rows)]
        copies = []
        if first:
            pl.semaphore_wait(barrier, len(F_PEERS) + len(D_PEERS))
        for o in peers:
            cp = pltpu.make_async_remote_copy(
                src_ref=mine, dst_ref=mine, send_sem=ssem.at[n], recv_sem=rsem.at[n],
                device_id=ident(o), device_id_type=MESH)
            cp.start()
            copies.append(cp)
        some = buf.at[n, pl.ds(0, count - 1), pl.ds(0, rows)]
        pltpu.make_async_copy(some, some, rsem.at[n]).wait()
        return some, ssem.at[n]

    def summed(buf, n, count, lo, hi):
        parts = [buf[n, k, pl.ds(lo, hi - lo), :] for k in range(count)]
        while len(parts) > 1:
            parts = [parts[i] + parts[i + 1] for i in range(0, len(parts), 2)]
        return parts[0]

    sent = []
    lhs = lhs_of(w_ref[...])
    for c in range(NCHUNK):
        loads[c].wait()
        rows = pl.ds(c * CHUNK, CHUNK)
        block = xf[rows, :]
        high = block.astype(jnp.bfloat16)
        low = (block - high.astype(jnp.float32)).astype(jnp.bfloat16)
        xh[rows, :] = high
        xl[rows, :] = low
        nt = ((1,), (1,))
        out = mult(lhs, high, nt) + mult(lhs, low, nt)
        to_slot(out, fbuf.at[0, feat], c * (CHUNK // LANES))
    sent.append(exchange(fbuf, 0, feat, NF, ROWS, F_PEERS, f_id, fs, fr, first=True))
    y = labels_ref[...].astype(jnp.float32)
    margin = y * summed(fbuf, 0, NF, 0, ROWS)
    sig = 1.0 / (1.0 + jnp.exp(-margin))
    curv = PENALTY * sig * (1.0 - sig)

    def back(u):
        lhs = lhs_of(u)
        nn = ((1,), (0,))
        return mult(lhs, xh[...], nn) + mult(lhs, xl[...], nn)

    def forward(v):
        lhs = lhs_of(v)
        nt = ((1,), (1,))
        return mult(lhs, xh[...], nt) + mult(lhs, xl[...], nt)

    to_slot(back((sig - 1.0) * y), dbuf.at[0, z], 0)
    sent.append(exchange(dbuf, 0, z, NZ, ROWS, D_PEERS, d_id, ds_, dr))
    gradient = w_ref[...] + PENALTY * summed(dbuf, 0, NZ, 0, ROWS)
    grad_ref[...] = gradient

    newton = jnp.zeros_like(gradient)
    residual = -gradient
    direction = residual
    image_rows = None
    rr = pp = None
    for step in range(1, CG_STEPS + 1):
        mine = fbuf.at[step, feat]
        to_slot(forward(residual), mine, 0)
        mine[pl.ds(ROWS, 1), :] = jnp.sum(residual * residual, axis=0, keepdims=True)
        if step > 1:
            mine[pl.ds(ROWS + 1, 1), :] = jnp.sum(residual * direction, axis=0, keepdims=True)
        nrows = ROWS + (1 if step == 1 else 2)
        sent.append(exchange(fbuf, step, feat, NF, nrows, F_PEERS, f_id, fs, fr))
        rows_r = summed(fbuf, step, NF, 0, ROWS)
        scal = jnp.sum(summed(fbuf, step, NF, ROWS, nrows), axis=1, keepdims=True)
        fresh = scal[0:1]
        if step == 1:
            image_rows = rows_r
            pp = fresh
        else:
            beta = fresh / rr
            direction = residual + beta * direction
            image_rows = rows_r + beta * image_rows
            pp = fresh + 2.0 * beta * scal[1:2] + beta * beta * pp
        rr = fresh
        weighted = curv * image_rows
        mine = dbuf.at[step, z]
        to_slot(back(weighted), mine, 0)
        mine[pl.ds(ROWS, 1), :] = jnp.sum(weighted * image_rows, axis=0, keepdims=True)
        sent.append(exchange(dbuf, step, z, NZ, ROWS + 1, D_PEERS, d_id, ds_, dr))
        image = direction + summed(dbuf, step, NZ, 0, ROWS)
        quad = jnp.sum(summed(dbuf, step, NZ, ROWS, ROWS + 1), axis=1, keepdims=True)
        alpha = rr / (pp + quad)
        newton = newton + alpha * direction
        residual = residual - alpha * image
    step_ref[...] = newton
    res_ref[...] = residual
    for some, sem in sent:
        pltpu.make_async_copy(some, some, sem).wait()


def local(features, labels, weights):
    vec = jax.ShapeDtypeStruct((ROWS, LANES), jnp.float32)
    vmem = pl.BlockSpec(memory_space=pltpu.VMEM)
    outs = pl.pallas_call(
        kernel,
        name="newton_cg",
        out_shape=(vec, vec, vec),
        in_specs=[pl.BlockSpec(memory_space=pltpu.HBM), vmem, vmem],
        out_specs=(vmem, vmem, vmem),
        scratch_shapes=[
            pltpu.VMEM((N, N), jnp.float32),
            pltpu.VMEM((N, N), jnp.bfloat16),
            pltpu.VMEM((N, N), jnp.bfloat16),
            pltpu.VMEM((CG_STEPS + 1, NF, SLOT, LANES), jnp.float32),
            pltpu.VMEM((CG_STEPS + 1, NZ, SLOT, LANES), jnp.float32),
            pltpu.SemaphoreType.DMA((NCHUNK,)),
            pltpu.SemaphoreType.DMA((CG_STEPS + 1,)),
            pltpu.SemaphoreType.DMA((CG_STEPS + 1,)),
            pltpu.SemaphoreType.DMA((CG_STEPS + 1,)),
            pltpu.SemaphoreType.DMA((CG_STEPS + 1,)),
        ],
        compiler_params=pltpu.CompilerParams(
            collective_id=0, has_side_effects=True, vmem_limit_bytes=62 * 1024 * 1024
        ),
    )(features, labels.reshape(ROWS, LANES), weights.reshape(ROWS, LANES))
    return tuple(o.reshape(N) for o in outs)


def solution(mesh):
    placed = (P("dp", "feat"), P("dp"), P("feat"))
    return jax.shard_map(
        local,
        mesh=mesh,
        in_specs=placed,
        out_specs=(P("feat"), P("feat"), P("feat")),
        check_vma=False,
    )
```

time: 197 us -> 59.9 us (0.30)
  blocking collectives: 92.4 us -> 0 us
  Pallas kernels: 0 us -> 55.2 us
  matrix products: 39.8 us -> 0 us
  waiting for transfers between devices: 19.9 us -> 0 us
  starting transfers between devices: 14.1 us -> 0 us
  other arithmetic: 11.9 us -> 0 us
  between operations: 9.5 us -> 0.64 us
  local copies, waits for them, and re-layouts: 8.1 us -> 3.8 us
    all_to_all x7 -> x0, blocking collectives: 92.4 us -> none  [sent_to_all(): lax.all_to_all(jnp.broadcast_to(value[None], (count, *value.shape)), axis...]
    pallas_call x0 -> x1, Pallas kernels: none -> 55.2 us  [local(): pl.pallas_call(kernel, name='newton_cg', out_shape=(vec, vec, vec), in_sp...]
    dot_general x8 -> x0, matrix products: 39.8 us -> none  [the longest x3 16.9 us: local(): jnp.dot(features, direction, precision=HIGH)]
    all_to_all x4 -> x0, waiting for transfers between devices: 19.9 us -> none  [sent_to_all(): lax.all_to_all(jnp.broadcast_to(value[None], (count, *value.shape)), axis...]
    all_to_all x4 -> x0, starting transfers between devices: 14.1 us -> none  [sent_to_all(): lax.all_to_all(jnp.broadcast_to(value[None], (count, *value.shape)), axis...]
    reduce_sum x19 -> x0, other arithmetic: 7.32 us -> none  [the longest x11 2.45 us: over_copies(): return sent_to_all(value, axis).sum(axis=0)]
    broadcast_in_dim x11 -> x0, local copies, waits for them, and re-layouts: 4.77 us -> none  [sent_to_all(): jnp.broadcast_to(value[None], (count, *value.shape))]
    concatenate x6 -> x0, other arithmetic: 3.94 us -> none  [together(): jnp.concatenate([a.reshape(-1) for a in arrays])]
  transfers between devices with their start and end apart: 4 -> 0, of which waited for: 4 -> 0; matrix products, arithmetic and copies ran while one was open for 4% -> 0% of each run, Pallas kernels for 0% -> 0%
where the time goes in v1:
time: 59.9 us; the launch traced here: 59.7 us
  Pallas kernels  55.2 us (92%)
  local copies, waits for them, and re-layouts  3.8 us (6%)
  between operations  0.64 us (1%)
    pallas_call x1, Pallas kernels, local(): pl.pallas_call(kernel, name='newton_cg', out_shape=(vec, vec, vec), in_sp...  55.2 us
    unnamed x3, local copies, waits for them, and re-layouts  3.8 us

profile of v1, /device:TPU:1, one launch (start us, length us, event | category | flops | bytes accessed | tf_op | source)
XLA Modules:
  0.0 59.7 jit_solution(1432099254229997531)
XLA Ops:
  0.6 55.2 %newton_cg.1 = (f32[8,128]{1,0:T(8,128)}, f32[8,128]{1,0:T(8,128)}, f32[8,128]{1,0:T(8,128)}) custom-call(f32[1024,1024]{1,0:T(8,128)} %x_hbm.1, s32[8,128]{1,0:T(8,128)} %bitcast.8, f32[8,128]{1,0:T(8,128)} %bitcast.9), custom_call_target="tpu_custom_call" | custom-call | tf_op jit(solution)/shard_map/newton_cg/pallas_call | solution.py:178
  55.9 1.3 %copy.9 = f32[1024]{0:T(1024)} copy(f32[1024]{0:T(1024)} %bitcast.7) | data formatting | bytes 8192
  57.1 1.3 %copy.10 = f32[1024]{0:T(1024)} copy(f32[1024]{0:T(1024)} %bitcast.6) | data formatting | bytes 8192
  58.4 1.3 %copy.11 = f32[1024]{0:T(1024)} copy(f32[1024]{0:T(1024)} %bitcast.5) | data formatting | bytes 8192

commit v2 on v1

--- a/solution.py
+++ b/solution.py
@@ -32,18 +32,22 @@
 D_PEERS = sorted(range(1, NZ), key=lambda d: -ring(d, NZ))
 
 
-def kernel(x_hbm, labels_ref, w_ref, grad_ref, step_ref, res_ref,
-           xf, xh, xl, fbuf, dbuf, xsem, fs, fr, ds_, dr):
+def kernel(x_hbm, labels_hbm, w_hbm, out_ref,
+           xf, xh, xl, labels_ref, w_ref, fbuf, dbuf, vsem, xsem, fs, fr, ds_, dr):
     feat = lax.axis_index("feat")
     z = lax.axis_index("dp")
     px, py, pc = feat // (NY * NC), (feat // NC) % NY, feat % NC
 
+    w_load = pltpu.make_async_copy(w_hbm, w_ref, vsem.at[0])
+    w_load.start()
     loads = []
     for c in range(NCHUNK):
         rows = pl.ds(c * CHUNK, CHUNK)
         cp = pltpu.make_async_copy(x_hbm.at[rows], xf.at[rows], xsem.at[c])
         cp.start()
         loads.append(cp)
+    labels_load = pltpu.make_async_copy(labels_hbm, labels_ref, vsem.at[1])
+    labels_load.start()
 
     def f_id(o):
         return {"feat": (((px + o[0]) % NX) * NY + (py + o[1]) % NY) * NC + (pc + o[2]) % NC}
@@ -98,6 +102,7 @@
         return parts[0]
 
     sent = []
+    w_load.wait()
     lhs = lhs_of(w_ref[...])
     for c in range(NCHUNK):
         loads[c].wait()
@@ -111,6 +116,7 @@
         out = mult(lhs, high, nt) + mult(lhs, low, nt)
         to_slot(out, fbuf.at[0, feat], c * (CHUNK // LANES))
     sent.append(exchange(fbuf, 0, feat, NF, ROWS, F_PEERS, f_id, fs, fr, first=True))
+    labels_load.wait()
     y = labels_ref[...].astype(jnp.float32)
     margin = y * summed(fbuf, 0, NF, 0, ROWS)
     sig = 1.0 / (1.0 + jnp.exp(-margin))
@@ -129,7 +135,7 @@
     to_slot(back((sig - 1.0) * y), dbuf.at[0, z], 0)
     sent.append(exchange(dbuf, 0, z, NZ, ROWS, D_PEERS, d_id, ds_, dr))
     gradient = w_ref[...] + PENALTY * summed(dbuf, 0, NZ, 0, ROWS)
-    grad_ref[...] = gradient
+    out_ref[0:8] = gradient
 
     newton = jnp.zeros_like(gradient)
     residual = -gradient
@@ -166,27 +172,30 @@
         alpha = rr / (pp + quad)
         newton = newton + alpha * direction
         residual = residual - alpha * image
-    step_ref[...] = newton
-    res_ref[...] = residual
+    out_ref[8:16] = newton
+    out_ref[16:24] = residual
     for some, sem in sent:
         pltpu.make_async_copy(some, some, sem).wait()
 
 
 def local(features, labels, weights):
-    vec = jax.ShapeDtypeStruct((ROWS, LANES), jnp.float32)
     vmem = pl.BlockSpec(memory_space=pltpu.VMEM)
+    hbm = pl.BlockSpec(memory_space=pltpu.HBM)
     outs = pl.pallas_call(
         kernel,
         name="newton_cg",
-        out_shape=(vec, vec, vec),
-        in_specs=[pl.BlockSpec(memory_space=pltpu.HBM), vmem, vmem],
-        out_specs=(vmem, vmem, vmem),
+        out_shape=pltpu.VMEM((3*ROWS, LANES), jnp.float32),
+        in_specs=[hbm, hbm, hbm],
+        out_specs=vmem,
         scratch_shapes=[
             pltpu.VMEM((N, N), jnp.float32),
             pltpu.VMEM((N, N), jnp.bfloat16),
             pltpu.VMEM((N, N), jnp.bfloat16),
+            pltpu.VMEM((ROWS, LANES), jnp.int32),
+            pltpu.VMEM((ROWS, LANES), jnp.float32),
             pltpu.VMEM((CG_STEPS + 1, NF, SLOT, LANES), jnp.float32),
             pltpu.VMEM((CG_STEPS + 1, NZ, SLOT, LANES), jnp.float32),
+            pltpu.SemaphoreType.DMA((2,)),
             pltpu.SemaphoreType.DMA((NCHUNK,)),
             pltpu.SemaphoreType.DMA((CG_STEPS + 1,)),
             pltpu.SemaphoreType.DMA((CG_STEPS + 1,)),
@@ -197,7 +206,8 @@
             collective_id=0, has_side_effects=True, vmem_limit_bytes=62 * 1024 * 1024
         ),
     )(features, labels.reshape(ROWS, LANES), weights.reshape(ROWS, LANES))
-    return tuple(o.reshape(N) for o in outs)
+    outs = outs.reshape(3, N)
+    return outs[0], outs[1], outs[2]
 
 
 def solution(mesh):

time: 59.9 us -> 55.4 us (0.925)
  local copies, waits for them, and re-layouts: 3.8 us -> 0.6 us
  Pallas kernels: 55.2 us -> 54.1 us
    unnamed x3 -> x0, local copies, waits for them, and re-layouts: 3.8 us -> none
    pallas_call x1, Pallas kernels: 55.2 us -> 54.1 us  [local(): pl.pallas_call(kernel, name='newton_cg', out_shape=pltpu.VMEM((3 * ROWS,...]
    squeeze x0 -> x1, local copies, waits for them, and re-layouts: none -> 0.6 us  [local(): return (outs[0], outs[1], outs[2])]
where the time goes in v2:
time: 55.4 us; the launch traced here: 55.3 us
  Pallas kernels  54.1 us (98%)
  between operations  0.64 us (1%)
  local copies, waits for them, and re-layouts  0.6 us (1%)
    pallas_call x1, Pallas kernels, local(): pl.pallas_call(kernel, name='newton_cg', out_shape=pltpu.VMEM((3 * ROWS,...  54.1 us

profile of v2, /device:TPU:1, one launch (start us, length us, event | category | flops | bytes accessed | tf_op | source)
XLA Modules:
  0.0 55.3 jit_solution(1899182242049205593)
XLA Ops:
  0.6 54.1 %newton_cg.1 = f32[24,128]{1,0:T(8,128)S(1)} custom-call(f32[1024,1024]{1,0:T(8,128)} %x_hbm.1, s32[8,128]{1,0:T(8,128)} %bitcast.8, f32[8,128]{1,0:T(8,128)} %bitcast.9), custom_call_target="tpu_custom_call" | custom-call | tf_op jit(solution)/shard_map/newton_cg/pallas_call | solution.py:184
  54.7 0.6 %slice_bitcast_fusion = (f32[1024]{0:T(1024)}, f32[1024]{0:T(1024)}, f32[1024]{0:T(1024)}) fusion(f32[24,128]{1,0:T(8,128)S(1)} %newton_cg.1), kind=kLoop, calls=%fused_computation | loop fusion | bytes 24576 | tf_op jit(solution)/shard_map/squeeze | solution.py:210
